TPU v7x, 32 devices: a whole 2x2x4 slice. The times are simulated.
32 devices in a mesh: dp: 4 (over z), row: 4 (over y, x), col: 2 (over core).
Axes of the slice: x: 2, y: 2, z: 4, core: 2. Of those that a mesh axis runs over, the one named last changes fastest.
Arguments:
- tokens: bfloat16 [4096, 1600], P(('dp', 'row'), 'col'), may hold values from -6 to 6
- segment_ids: int32 [4, 1024], P('dp'), may hold values from 0 to 3, as said below
- first_gain: float32 [1600], replicated, may hold values from 0.1 to 1.9
- first_shift: float32 [1600], replicated, may hold values from -3 to 3
- triple_weight: bfloat16 [1600, 4800], P('col', 'row'), may hold values from -1 to 1
- query_bias: float32 [1600], replicated, may hold values from -3 to 3
- value_bias: float32 [1600], replicated, may hold values from -3 to 3
- proj_weight: bfloat16 [1600, 1600], P('row', 'col'), may hold values from -0.4375 to 0.4375
- proj_bias: float32 [1600], replicated, may hold values from -3 to 3
- second_gain: float32 [1600], replicated, may hold values from 0.1 to 1.9
- second_shift: float32 [1600], replicated, may hold values from -3 to 3
- expand_weight: bfloat16 [1600, 6400], P('col', 'row'), may hold values from -0.15625 to 0.15625
- expand_bias: float32 [6400], replicated, may hold values from -3 to 3
- shrink_weight: bfloat16 [6400, 1600], P('row', 'col'), may hold values from -0.078125 to 0.078125
- shrink_bias: float32 [1600], replicated, may hold values from -3 to 3
- cotangent: bfloat16 [4096, 1600], P(('dp', 'row'), 'col'), may hold values from -6 to 6
Outputs:
- block_out: bfloat16 [4096, 1600], P(('dp', 'row'), 'col')
- input_grad: float32 [4096, 1600], P(('dp', 'row'), 'col')
- first_gain_grad: float32 [1600], replicated
- first_shift_grad: float32 [1600], replicated
- triple_grad: float32 [2, 800, 4800], P('col', 'dp', 'row')
- query_bias_grad: float32 [1600], replicated
- value_bias_grad: float32 [1600], replicated
- proj_grad: float32 [4, 400, 1600], P('row', 'dp', 'col')
- proj_bias_grad: float32 [1600], replicated
- second_gain_grad: float32 [1600], replicated
- second_shift_grad: float32 [1600], replicated
- expand_grad: float32 [2, 800, 6400], P('col', 'dp', 'row')
- expand_bias_grad: float32 [6400], replicated
- shrink_grad: float32 [4, 1600, 1600], P('row', 'dp', 'col')
- shrink_bias_grad: float32 [1600], replicated
Inputs may be any that keep to these rules, and one draw needn't show every extreme that they name: `segment_ids`: each row lists the sequences of one data group in order: it starts at 0 and rises by one where a new sequence starts. A row holds 1 to 4 sequences; in every draw some row holds exactly 4 and another holds a single sequence of 1024 tokens.
All inputs are finite; a program needn't handle non-finite values.
Results may differ from a plain program's by a relative error of at most 0.014.
Values may be sent and summed in bfloat16 or wider, within the bound.
A program may use at most 192 MiB of HBM per device.

v0:
```python
import math
import jax
import jax.numpy as jnp
from jax import lax
from jax.sharding import PartitionSpec as P

HEADS = 25
HEAD_DIM = 64
FF = 6400
EPS = 1e-05
NEG = -1e30


def gelu_tanh(values):
    return (
        0.5
        * values
        * (1.0 + jnp.tanh(0.7978845608028654 * (values + 0.044715 * values * values * values)))
    )


def spread_rows(own_part):
    return lax.all_gather(own_part, "row", axis=0, tiled=True)


def reduce_cols(partial_sum):
    return lax.psum_scatter(partial_sum, "col", scatter_dimension=0, tiled=True)


def spread_cols(own_part):
    return lax.all_gather(own_part, "col", axis=0, tiled=True)


def reduce_rows(partial_sum):
    return lax.psum_scatter(partial_sum, "row", scatter_dimension=0, tiled=True)


def to_heads(hidden):
    return lax.all_to_all(hidden, "row", split_axis=0, concat_axis=1, tiled=True)


def to_hidden(headed):
    return lax.all_to_all(headed, "row", split_axis=1, concat_axis=0, tiled=True)


def gather_keys(own_part):
    return lax.all_gather(own_part, ("row", "col"), axis=0, tiled=True)


def feature_totals(first_term, second_term):
    return lax.psum(
        (jnp.sum(first_term, axis=1, keepdims=True), jnp.sum(second_term, axis=1, keepdims=True)),
        "col",
    )


def norm_local(matrix, gain, shift):
    width = HEADS * HEAD_DIM
    total, square = feature_totals(matrix, matrix * matrix)
    average = total / width
    rstd = lax.rsqrt(square / width - average * average + EPS)
    normed_hat = (matrix - average) * rstd
    return (normed_hat * gain + shift, normed_hat, rstd)


def norm_back(grad_in, normed_hat, rstd, gain):
    width = HEADS * HEAD_DIM
    scaled = grad_in * gain
    total, mixed = feature_totals(scaled, scaled * normed_hat)
    return rstd * (scaled - total / width - normed_hat * mixed / width)


def head_split(matrix):
    rows = matrix.shape[0]
    group_size = math.gcd(HEADS, 5)
    return matrix.reshape(rows, HEADS // group_size, group_size, HEAD_DIM).transpose(1, 0, 2, 3)


def head_join(blocks):
    rows = blocks.shape[1]
    return blocks.transpose(1, 0, 2, 3).reshape(rows, HEADS * HEAD_DIM)


def attention_forward(query_part, key_part, value_part, allowed):
    scaling = HEAD_DIM ** (-0.5)

    def one_group(blocks):
        query_block, key_block, value_block = blocks
        scores = (
            jnp.einsum("qhd,khd->hqk", query_block, key_block, preferred_element_type=jnp.float32)
            * scaling
        )
        scores = jnp.where(allowed[None], scores, NEG)
        highest = jnp.max(scores, axis=-1)
        log_total = highest + jnp.log(jnp.sum(jnp.exp(scores - highest[..., None]), axis=-1))
        weights = jnp.exp(scores - log_total[..., None]).astype(jnp.bfloat16)
        combined = jnp.einsum(
            "hqk,khd->qhd", weights, value_block, preferred_element_type=jnp.float32
        ).astype(jnp.bfloat16)
        return (combined, log_total)

    combined, log_total = lax.map(
        one_group, (head_split(query_part), head_split(key_part), head_split(value_part))
    )
    return (head_join(combined), log_total)


def attention_backward(
    query_part, key_part, value_part, attended, attended_grad, log_total, allowed
):
    scaling = HEAD_DIM ** (-0.5)

    def one_group(blocks):
        query_block, key_block, value_block, out_block, grad_block, lse_block = blocks
        scores = (
            jnp.einsum("qhd,khd->hqk", query_block, key_block, preferred_element_type=jnp.float32)
            * scaling
        )
        scores = jnp.where(allowed[None], scores, NEG)
        weights = jnp.exp(scores - lse_block[..., None])
        weights_half = weights.astype(jnp.bfloat16)
        value_grad = jnp.einsum(
            "hqk,qhd->khd", weights_half, grad_block, preferred_element_type=jnp.float32
        )
        weight_grad = jnp.einsum(
            "qhd,khd->hqk", grad_block, value_block, preferred_element_type=jnp.float32
        )
        delta = jnp.sum(
            grad_block.astype(jnp.float32) * out_block.astype(jnp.float32), axis=-1
        ).transpose(1, 0)
        mix_half = (weights * (weight_grad - delta[..., None])).astype(jnp.bfloat16)
        query_grad = (
            jnp.einsum("hqk,khd->qhd", mix_half, key_block, preferred_element_type=jnp.float32)
            * scaling
        )
        key_grad = (
            jnp.einsum("hqk,qhd->khd", mix_half, query_block, preferred_element_type=jnp.float32)
            * scaling
        )
        return (query_grad, key_grad, value_grad)

    query_grad, key_grad, value_grad = lax.map(
        one_group,
        (
            head_split(query_part),
            head_split(key_part),
            head_split(value_part),
            head_split(attended),
            head_split(attended_grad),
            log_total,
        ),
    )
    return (head_join(query_grad), head_join(key_grad), head_join(value_grad))


def shards(
    tokens,
    segment_ids,
    first_gain,
    first_shift,
    triple_weight,
    query_bias,
    value_bias,
    proj_weight,
    proj_bias,
    second_gain,
    second_shift,
    expand_weight,
    expand_bias,
    shrink_weight,
    shrink_bias,
    cotangent,
):
    width = HEADS * HEAD_DIM
    row_count = lax.axis_size("row")
    col_count = lax.axis_size("col")
    row_index = lax.axis_index("row")
    col_index = lax.axis_index("col")
    col_width = tokens.shape[1]
    group_rows = segment_ids.shape[1]
    query_rows = group_rows // (row_count * col_count)
    hidden_width = expand_weight.shape[1]
    triple_width = triple_weight.shape[1]

    def col_slice(vector):
        return lax.dynamic_slice_in_dim(vector, col_index * col_width, col_width)

    def col_place(vector):
        return lax.dynamic_update_slice_in_dim(
            jnp.zeros((width,), jnp.float32), vector, col_index * col_width, 0
        )

    tokens_wide = tokens.astype(jnp.float32)
    first_normed, first_hat, first_rstd = norm_local(
        tokens_wide, col_slice(first_gain), col_slice(first_shift)
    )
    first_half = first_normed.astype(jnp.bfloat16)
    first_all = spread_rows(first_half)
    full_bias = jnp.concatenate([query_bias, jnp.zeros((width,), jnp.float32), value_bias])
    triple_sum = reduce_cols(jnp.dot(first_all, triple_weight, preferred_element_type=jnp.float32))
    triple_local = (
        triple_sum + lax.dynamic_slice_in_dim(full_bias, row_index * triple_width, triple_width)
    ).astype(jnp.bfloat16)
    headed = to_heads(triple_local)
    query_part = headed[:, :width]
    pair_local = headed[:, width:]
    pair_all = gather_keys(pair_local)
    segment_row = segment_ids[0]
    query_start = col_index * (group_rows // col_count) + row_index * query_rows
    query_places = query_start + jnp.arange(query_rows, dtype=jnp.int32)
    query_segments = lax.dynamic_slice_in_dim(segment_row, query_start, query_rows)
    key_places = (
        jnp.arange(group_rows, dtype=jnp.int32)
        .reshape(col_count, row_count, query_rows)
        .transpose(1, 0, 2)
        .reshape(group_rows)
    )
    key_segments = (
        segment_row.reshape(col_count, row_count, query_rows).transpose(1, 0, 2).reshape(group_rows)
    )
    allowed = (query_segments[:, None] == key_segments[None, :]) & (
        key_places[None, :] <= query_places[:, None]
    )
    attended, log_total = attention_forward(
        query_part, pair_all[:, :width], pair_all[:, width:], allowed
    )
    attended_hidden = to_hidden(attended)
    attended_all = spread_cols(attended_hidden)
    middle = (
        tokens_wide
        + reduce_rows(jnp.dot(attended_all, proj_weight, preferred_element_type=jnp.float32))
        + col_slice(proj_bias)
    )
    second_normed, second_hat, second_rstd = norm_local(
        middle, col_slice(second_gain), col_slice(second_shift)
    )
    second_half = second_normed.astype(jnp.bfloat16)
    second_all = spread_rows(second_half)
    before_act = reduce_cols(
        jnp.dot(second_all, expand_weight, preferred_element_type=jnp.float32)
    ) + lax.dynamic_slice_in_dim(expand_bias, row_index * hidden_width, hidden_width)
    activated = gelu_tanh(before_act).astype(jnp.bfloat16)
    activated_all = spread_cols(activated)
    block_out = (
        middle
        + reduce_rows(jnp.dot(activated_all, shrink_weight, preferred_element_type=jnp.float32))
        + col_slice(shrink_bias)
    ).astype(jnp.bfloat16)
    pair_back = gather_keys(pair_local)
    activated_back = spread_cols(activated)
    second_back = spread_rows(second_half)
    attended_back = spread_cols(attended_hidden)
    first_back = spread_rows(first_half)
    cot_wide = cotangent.astype(jnp.float32)
    cot_all = spread_rows(cotangent)
    shrink_grad = jnp.einsum(
        "tf,td->fd", activated_back, cot_all, preferred_element_type=jnp.float32
    )
    shrink_bias_part = jnp.sum(cot_wide, axis=0)
    act_grad = reduce_cols(
        jnp.einsum("td,fd->tf", cot_all, shrink_weight, preferred_element_type=jnp.float32)
    )
    gelu_back = jax.vjp(gelu_tanh, before_act)[1]
    before_grad = gelu_back(act_grad)[0]
    expand_bias_part = jnp.sum(before_grad, axis=0)
    hidden_grad = before_grad.astype(jnp.bfloat16)
    hidden_all = spread_cols(hidden_grad)
    expand_grad = jnp.einsum(
        "td,tf->df", second_back, hidden_all, preferred_element_type=jnp.float32
    )
    second_normed_grad = reduce_rows(
        jnp.einsum("tf,df->td", hidden_all, expand_weight, preferred_element_type=jnp.float32)
    )
    middle_grad = cot_wide + norm_back(
        second_normed_grad, second_hat, second_rstd, col_slice(second_gain)
    )
    second_gain_part = jnp.sum(second_normed_grad * second_hat, axis=0)
    second_shift_part = jnp.sum(second_normed_grad, axis=0)
    middle_half = middle_grad.astype(jnp.bfloat16)
    middle_all = spread_rows(middle_half)
    proj_grad = jnp.einsum(
        "tc,td->cd", attended_back, middle_all, preferred_element_type=jnp.float32
    )
    proj_bias_part = jnp.sum(middle_grad, axis=0)
    attended_grad_hidden = reduce_cols(
        jnp.einsum("td,cd->tc", middle_all, proj_weight, preferred_element_type=jnp.float32)
    ).astype(jnp.bfloat16)
    attended_grad = to_heads(attended_grad_hidden)
    query_grad, key_grad, value_grad = attention_backward(
        query_part,
        pair_back[:, :width],
        pair_back[:, width:],
        attended,
        attended_grad,
        log_total,
        allowed,
    )
    pair_grad = lax.psum_scatter(
        jnp.concatenate([key_grad, value_grad], axis=1).astype(jnp.bfloat16),
        ("row", "col"),
        scatter_dimension=0,
        tiled=True,
    ).astype(jnp.float32)
    query_bias_part = jnp.sum(query_grad, axis=0)
    value_bias_part = jnp.sum(pair_grad[:, width:], axis=0)
    triple_half = jnp.concatenate([query_grad, pair_grad], axis=1).astype(jnp.bfloat16)
    triple_hidden = to_hidden(triple_half)
    triple_all = spread_cols(triple_hidden)
    triple_grad = jnp.einsum(
        "tc,tk->ck", first_back, triple_all, preferred_element_type=jnp.float32
    )
    first_normed_grad = reduce_rows(
        jnp.einsum("tk,ck->tc", triple_all, triple_weight, preferred_element_type=jnp.float32)
    )
    input_grad = middle_grad + norm_back(
        first_normed_grad, first_hat, first_rstd, col_slice(first_gain)
    )
    first_gain_part = jnp.sum(first_normed_grad * first_hat, axis=0)
    first_shift_part = jnp.sum(first_normed_grad, axis=0)
    shrink_owned, expand_owned, proj_owned, triple_owned = (
        lax.psum_scatter(
            shrink_grad.astype(jnp.bfloat16), "dp", scatter_dimension=0, tiled=True
        ).astype(jnp.float32),
        lax.psum_scatter(
            expand_grad.astype(jnp.bfloat16), "dp", scatter_dimension=0, tiled=True
        ).astype(jnp.float32),
        lax.psum_scatter(
            proj_grad.astype(jnp.bfloat16), "dp", scatter_dimension=0, tiled=True
        ).astype(jnp.float32),
        lax.psum_scatter(
            triple_grad.astype(jnp.bfloat16), "dp", scatter_dimension=0, tiled=True
        ).astype(jnp.float32),
    )
    expand_bias_full = lax.dynamic_update_slice_in_dim(
        jnp.zeros((FF,), jnp.float32), expand_bias_part, row_index * hidden_width, 0
    )
    (
        first_gain_grad,
        first_shift_grad,
        query_bias_grad,
        value_bias_grad,
        proj_bias_grad,
        second_gain_grad,
        second_shift_grad,
        expand_bias_grad,
        shrink_bias_grad,
    ) = lax.psum(
        (
            col_place(first_gain_part),
            col_place(first_shift_part),
            query_bias_part,
            value_bias_part,
            col_place(proj_bias_part),
            col_place(second_gain_part),
            col_place(second_shift_part),
            expand_bias_full,
            col_place(shrink_bias_part),
        ),
        ("dp", "row", "col"),
    )
    return (
        block_out,
        input_grad,
        first_gain_grad,
        first_shift_grad,
        triple_owned[None],
        query_bias_grad,
        value_bias_grad,
        proj_owned[None],
        proj_bias_grad,
        second_gain_grad,
        second_shift_grad,
        expand_owned[None],
        expand_bias_grad,
        shrink_owned[None],
        shrink_bias_grad,
    )


def solution(mesh):
    in_specs = (
        P(("dp", "row"), "col"),
        P("dp", None),
        P(),
        P(),
        P("col", "row"),
        P(),
        P(),
        P("row", "col"),
        P(),
        P(),
        P(),
        P("col", "row"),
        P(),
        P("row", "col"),
        P(),
        P(("dp", "row"), "col"),
    )
    out_specs = (
        P(("dp", "row"), "col"),
        P(("dp", "row"), "col"),
        P(),
        P(),
        P("col", "dp", "row"),
        P(),
        P(),
        P("row", "dp", "col"),
        P(),
        P(),
        P(),
        P("col", "dp", "row"),
        P(),
        P("row", "dp", "col"),
        P(),
    )
    return jax.shard_map(shards, mesh=mesh, in_specs=in_specs, out_specs=out_specs, check_vma=False)
```

profile of v0, /device:TPU:8, one launch (start us, length us, event | category | flops | bytes accessed | tf_op | source)
XLA Modules:
  0.0 1063.2 jit_solution(4812785820477544003)
XLA Ops:
  14.7 32.5 %all-gather.9.cloned.1.call-done = bf16[1024,800]{0,1:T(8,128)(2,1)} async-done(((bf16[256,800]{0,1:T(8,128)(2,1)}), bf16[1024,800]{0,1:T(8,128)(2,1)}) %all-gather.9.cloned.1.call-update) | async-done | bytes 1638416 | tf_op jit(solution)/shard_map/all_gather | solution.py:23
  55.1 12.2 %reduce-scatter.19.cloned.1.call-done = f32[512,1200]{0,1:T(8,128)} async-done(((f32[1024,1200]{0,1:T(8,128)}), f32[512,1200]{0,1:T(8,128)}) %reduce-scatter.19.cloned.1.call-update) | async-done | bytes 2457616 | tf_op jit(solution)/shard_map/reduce_scatter | solution.py:27
  69.2 20.1 %all_to_all.70 = bf16[4,128,1200]{1,2,0:T(8,128)(2,1)S(1)} all-to-all(bf16[4,128,1200]{1,2,0:T(8,128)(2,1)S(1)} %copy_bitcast_fusion.1), channel_id=1, replica_groups=mesh['dp'=4,'row'=4,'col'=2] {'row'}, dimensions={0} | all-to-all | bytes 2457600 | tf_op jit(solution)/shard_map/all_to_all | solution.py:39
  92.5 45.9 %all-gather.11.cloned.1.call-done = bf16[1024,3200]{0,1:T(8,128)(2,1)} async-done(((bf16[128,3200]{0,1:T(8,128)(2,1)}), bf16[1024,3200]{0,1:T(8,128)(2,1)}) %all-gather.11.cloned.1.call-update) | async-done | bytes 6553616 | tf_op jit(solution)/shard_map/all_gather | solution.py:47
  144.8 23.5 %while.28 = (s32[]{:T(128)}, bf16[5,128,5,64]{1,3,2,0:T(8,128)(2,1)S(1)}, f32[5,5,128]{2,1,0:T(8,128)S(1)}, bf16[5,1024,5,64]{1,3,2,0:T(8,128)(2,1)}, bf16[5,128...) while((s32[]{:T(128)}, ...), condition=%wide.region_8.9_spmd.clone, body=%wide.region_5.8_spmd.clone.sunk | while | flops 175414656 | bytes 9902713 | solution.py:102
  168.3 10.8 %all_to_all.71 = bf16[128,4,400]{0,2,1:T(8,128)(2,1)S(1)} all-to-all(bf16[128,4,400]{0,2,1:T(8,128)(2,1)S(1)} %bitcast.232), channel_id=1, replica_groups=mesh['dp'=4,'row'=4,'col'=2] {'row'}, dimensions={1} | all-to-all | bytes 819200 | tf_op jit(solution)/shard_map/all_to_all | solution.py:43
  186.1 43.4 %reduce-scatter.21.cloned.1.call-done = f32[256,800]{0,1:T(8,128)} async-done(((f32[1024,800]{0,1:T(8,128)}), f32[256,800]{0,1:T(8,128)}) %reduce-scatter.21.cloned.1.call-update) | async-done | bytes 819216 | tf_op jit(solution)/shard_map/reduce_scatter | solution.py:35
  236.2 26.2 %all-gather.17.cloned.1.call-done = bf16[1024,800]{0,1:T(8,128)(2,1)} async-done(((bf16[256,800]{0,1:T(8,128)(2,1)}), bf16[1024,800]{0,1:T(8,128)(2,1)}) %all-gather.17.cloned.1.call-update) | async-done | bytes 1638416 | tf_op jit(solution)/shard_map/all_gather | solution.py:23
  271.0 24.9 %all-gather.13.cloned.1.call-done = bf16[1024,800]{0,1:T(8,128)(2,1)} async-done(((bf16[256,800]{0,1:T(8,128)(2,1)}), bf16[1024,800]{0,1:T(8,128)(2,1)}) %all-gather.13.cloned.1.call-update) | async-done | bytes 1638416 | tf_op jit(solution)/shard_map/all_gather | solution.py:23
  312.7 17.7 %reduce-scatter.23.cloned.1.call-done = f32[512,1600]{0,1:T(8,128)} async-done(((f32[1024,1600]{0,1:T(8,128)}), f32[512,1600]{0,1:T(8,128)}) %reduce-scatter.23.cloned.1.call-update) | async-done | bytes 3276816 | tf_op jit(solution)/shard_map/reduce_scatter | solution.py:27
  337.5 13.0 %all-gather.19.cloned.1.call-done = bf16[1024,1600]{0,1:T(8,128)(2,1)} async-done(((bf16[512,1600]{0,1:T(8,128)(2,1)}), bf16[1024,1600]{0,1:T(8,128)(2,1)}) %all-gather.19.cloned.1.call-update) | async-done | bytes 3276816 | tf_op jit(solution)/shard_map/all_gather | solution.py:31
  372.9 41.4 %reduce-scatter.29.cloned.1.call-done = f32[256,800]{0,1:T(8,128)} async-done(((f32[1024,800]{0,1:T(8,128)}), f32[256,800]{0,1:T(8,128)}) %reduce-scatter.29.cloned.1.call-update) | async-done | bytes 819216 | tf_op jit(solution)/shard_map/reduce_scatter | solution.py:35
  418.5 43.8 %reduce-scatter.25.cloned.1.call-done = f32[256,800]{0,1:T(8,128)} async-done(((f32[1024,800]{0,1:T(8,128)}), f32[256,800]{0,1:T(8,128)}) %reduce-scatter.25.cloned.1.call-update) | async-done | bytes 819216 | tf_op jit(solution)/shard_map/reduce_scatter | solution.py:35
  465.9 31.4 %all-gather.21.cloned.1.call-done = bf16[1024,800]{0,1:T(8,128)(2,1)} async-done(((bf16[256,800]{0,1:T(8,128)(2,1)}), bf16[1024,800]{0,1:T(8,128)(2,1)}) %all-gather.21.cloned.1.call-update) | async-done | bytes 1638416 | tf_op jit(solution)/shard_map/all_gather | solution.py:23
  500.9 9.5 reduce-scatter.31.cloned.1.call-done
  523.2 52.5 %while.29 = (s32[]{:T(128)}, f32[5,128,5,64]{1,3,2,0:T(8,128)S(1)}, bf16[5,1024,5,64]{1,3,2,0:T(8,128)(2,1)}, bf16[5,1024,5,64]{1,3,2,0:T(8,128)(2,1)}, bf16[5,1...) while((s32[]{:T(128)}, f32[5,128,5,64]{1,3,2,0:T(8,128)S(1)}, ...), condition=%wide.region_25.26_spmd.clone, body=%wide.region_23.25_spmd.clone.sunk | while | flops 426909056 | bytes 17467036 | solution.py:142
  591.8 63.0 %reduce-scatter.39.cloned.1.call-done = bf16[128,3200]{1,0:T(8,128)(2,1)} async-done(((bf16[1024,3200]{1,0:T(8,128)(2,1)}), bf16[128,3200]{1,0:T(8,128)(2,1)}) %reduce-scatter.39.cloned.1.call-update) | async-done | bytes 819216
  656.7 18.8 %all_to_all.72 = bf16[128,4,1200]{0,2,1:T(8,128)(2,1)S(1)} all-to-all(bf16[128,4,1200]{0,2,1:T(8,128)(2,1)S(1)} %bitcast.226), channel_id=1, replica_groups=mesh['dp'=4,'row'=4,'col'=2] {'row'}, dimensions={1} | all-to-all | bytes 2457600 | tf_op jit(solution)/shard_map/all_to_all | solution.py:43
  707.7 35.1 %reduce-scatter.41.cloned.1.call-done = bf16[200,1600]{1,0:T(8,128)(2,1)} async-done(((bf16[800,1600]{1,0:T(8,128)(2,1)}), bf16[200,1600]{1,0:T(8,128)(2,1)}) %reduce-scatter.41.cloned.1.call-update) | async-done | bytes 640016
  747.6 36.1 %fusion.4 = bf16[112,800]{1,0:T(8,128)(2,1)S(1)} fusion(bf16[400,800]{1,0:T(8,128)(2,1)S(1)} %convolution_convert_fusion.3), kind=kCustom, calls=%all-reduce-scatter | all-reduce-scatter fusion | flops 358401 | bytes 819712
  788.3 25.3 %reduce-scatter.37.cloned.1.call-done = bf16[400,800]{1,0:T(8,128)(2,1)} async-done(((bf16[1600,800]{1,0:T(8,128)(2,1)}), bf16[400,800]{1,0:T(8,128)(2,1)}) %reduce-scatter.37.cloned.1.call-update) | async-done | bytes 640016 | tf_op jit(solution)/shard_map/reduce_scatter | solution.py:321
  820.5 39.6 %reduce-scatter.35.cloned.1.call-done = bf16[200,1200]{1,0:T(8,128)(2,1)} async-done(((bf16[800,1200]{1,0:T(8,128)(2,1)}), bf16[200,1200]{1,0:T(8,128)(2,1)}) %reduce-scatter.35.cloned.1.call-update) | async-done | bytes 480016 | tf_op jit(solution)/shard_map/reduce_scatter | solution.py:330
  862.3 45.7 %reduce-scatter.33.cloned.1.call-done = f32[256,800]{0,1:T(8,128)} async-done(((f32[1024,800]{0,1:T(8,128)}), f32[256,800]{0,1:T(8,128)}) %reduce-scatter.33.cloned.1.call-update) | async-done | bytes 819216 | tf_op jit(solution)/shard_map/reduce_scatter | solution.py:35
  915.9 128.6 %all-reduce.10.cloned.1.call-done = (f32[1600]{0:T(1024)}, f32[1600]{0:T(1024)}, f32[1600]{0:T(1024)}, f32[1600]{0:T(1024)}, f32[1600]{0:T(1024)}, /*index=5*/f3...) async-done(((f32[1600]{0:T(1024)}, f32[1600]{0:T(1024)}, f32[1600]{0:T(1024)}, f32[1600]{0:T(1024)}, f32[1600]{0:T(1024)}, /*index=5*/f32[1600]{0:T(1024)}, ...) | async-done | bytes 76816 | tf_op jit(solution)/shard_map/psum | solution.py:347
  (280 shorter events, 282.3 us)
Async XLA Ops:
  7.2 288.7 %copy-start = (bf16[800,1600]{1,0:T(8,128)(2,1)S(1)}, bf16[800,1600]{1,0:T(8,128)(2,1)}, u32[]{:S(2)}) copy-start(bf16[800,1600]{1,0:T(8,128)(2,1)} %param.31) | copy-start | bytes 7680004
  7.2 40.0 %all-gather.9.cloned.1.call-start = ((), (), s32[]{:S(2)}) async-start(), calls=%async_computation.16 | async-start | bytes 2048000 | tf_op jit(solution)/shard_map/all_gather | solution.py:23
  14.6 52.6 %reduce-scatter.19.cloned.1.call-start = ((), (), s32[]{:S(2)}) async-start(), calls=%async_computation.17 | async-start | bytes 7372800 | tf_op jit(solution)/shard_map/reduce_scatter | solution.py:27
  54.2 84.2 %all-gather.11.cloned.1.call-start = ((), (), s32[]{:S(2)}) async-start(), calls=%async_computation.18 | async-start | bytes 7372800 | tf_op jit(solution)/shard_map/all_gather | solution.py:47
  91.3 138.1 %reduce-scatter.21.cloned.1.call-start = ((), (), s32[]{:S(2)}) async-start(), calls=%async_computation.19 | async-start | bytes 4096000 | tf_op jit(solution)/shard_map/reduce_scatter | solution.py:35
  185.2 77.2 %all-gather.17.cloned.1.call-start = ((), (), s32[]{:S(2)}) async-start(), calls=%async_computation.24 | async-start | bytes 2048000 | tf_op jit(solution)/shard_map/all_gather | solution.py:23
  185.7 110.2 %all-gather.13.cloned.1.call-start = ((), (), s32[]{:S(2)}) async-start(), calls=%async_computation.20 | async-start | bytes 2048000 | tf_op jit(solution)/shard_map/all_gather | solution.py:23
  235.7 77.0 %reduce-scatter.27.cloned.1.call-start = ((), (), s32[]{:S(2)}) async-start(), calls=%async_computation.25 | async-start | bytes 9830400 | tf_op jit(solution)/shard_map/reduce_scatter | solution.py:27
  271.0 59.3 %reduce-scatter.23.cloned.1.call-start = ((), (), s32[]{:S(2)}) async-start(), calls=%async_computation.21 | async-start | bytes 9830400 | tf_op jit(solution)/shard_map/reduce_scatter | solution.py:27
  303.7 46.8 %all-gather.19.cloned.1.call-start = ((), (), s32[]{:S(2)}) async-start(), calls=%async_computation.26 | async-start | bytes 4915200 | tf_op jit(solution)/shard_map/all_gather | solution.py:31
  336.8 28.6 %all-gather.15.cloned.1.call-start = ((), (), s32[]{:S(2)}) async-start(), calls=%async_computation.22 | async-start | bytes 4915200 | tf_op jit(solution)/shard_map/all_gather | solution.py:31
  337.4 76.9 %reduce-scatter.29.cloned.1.call-start = ((), (), s32[]{:S(2)}) async-start(), calls=%async_computation.27 | async-start | bytes 4096000 | tf_op jit(solution)/shard_map/reduce_scatter | solution.py:35
  357.2 105.0 %reduce-scatter.25.cloned.1.call-start = ((), (), s32[]{:S(2)}) async-start(), calls=%async_computation.23 | async-start | bytes 4096000 | tf_op jit(solution)/shard_map/reduce_scatter | solution.py:35
  372.2 125.0 %all-gather.21.cloned.1.call-start = ((), (), s32[]{:S(2)}) async-start(), calls=%async_computation.28 | async-start | bytes 2048000 | tf_op jit(solution)/shard_map/all_gather | solution.py:23
  465.8 44.6 %reduce-scatter.31.cloned.1.call-start = ((), (), s32[]{:S(2)}) async-start(), calls=%async_computation.29 | async-start | bytes 2457600 | tf_op jit(solution)/shard_map/reduce_scatter | solution.py:27
  512.4 10.8 %all-to-all-start.2 = ((bf16[4,128,400]{1,2,0:T(8,128)(2,1)}), bf16[4,128,400]{1,2,0:T(8,128)(2,1)S(1)}, u32[]{:S(2)}, u32[]{:S(2)}) async-start(bf16[4,128,400]{1,2,0:T(8,128)(2,1)} %copy_bitcast_fusion.3), calls=%async_computation.9 | async-start | bytes 819200 | tf_op jit(solution)/shard_map/all_to_all | solution.py:39
  516.0 138.8 %reduce-scatter.39.cloned.1.call-start = ((), (), s32[]{:S(2)}) async-start(), calls=%async_computation.34 | async-start | bytes 7372800
  591.7 100.7 %all-gather.23.cloned.1.call-start = ((), (), s32[]{:S(2)}) async-start(), calls=%async_computation.30 | async-start | bytes 3686400 | tf_op jit(solution)/shard_map/all_gather | solution.py:31
  676.6 66.3 %reduce-scatter.41.cloned.1.call-start = ((), (), s32[]{:S(2)}) async-start(), calls=%async_computation.35 | async-start | bytes 3328000
  683.8 129.8 %reduce-scatter.37.cloned.1.call-start = ((), (), s32[]{:S(2)}) async-start(), calls=%async_computation.33 | async-start | bytes 3584000 | tf_op jit(solution)/shard_map/reduce_scatter | solution.py:321
  692.3 167.7 %reduce-scatter.35.cloned.1.call-start = ((), (), s32[]{:S(2)}) async-start(), calls=%async_computation.32 | async-start | bytes 2560000 | tf_op jit(solution)/shard_map/reduce_scatter | solution.py:330
  699.2 208.8 %reduce-scatter.33.cloned.1.call-start = ((), (), s32[]{:S(2)}) async-start(), calls=%async_computation.31 | async-start | bytes 4096000 | tf_op jit(solution)/shard_map/reduce_scatter | solution.py:35
  705.5 338.9 %all-reduce.10.cloned.1.call-start = ((), (), s32[]{:S(2)}) async-start(), calls=%async_computation.36 | async-start | bytes 188416 | tf_op jit(solution)/shard_map/psum | solution.py:347
  783.8 33.2 %collective-permute-start = (bf16[36,800]{1,0:T(8,128)(2,1)S(1)}, bf16[36,800]{1,0:T(8,128)(2,1)S(1)}, u32[]{:S(2)}, u32[]{:S(2)}) collective-permute-start(bf16[36,800]{1,0:T(8,128)(2,1)S(1)} %slice.31), channel_id=1, source_target_pairs={{0,8},{8,16},{16,24},{1,9},{9,17},{17,25},{2,10},{10,18},{18,26},{... | collective-permute-start | bytes 172808
  (34 other events, 1158.7 us)
Sparse Core Ops, SparseCore 0:
  14.7 32.3 all-gather.8
  54.3 12.8 reduce-scatter.18
  91.4 46.9 all-gather.10
  185.3 44.1 reduce-scatter.20
  231.1 31.2 all-gather.16
  264.6 31.2 all-gather.12
  298.2 14.4 reduce-scatter.26
  315.0 15.3 reduce-scatter.22
  337.0 13.4 all-gather.18
  351.9 13.4 all-gather.14
  368.4 45.8 reduce-scatter.28
  417.2 44.9 reduce-scatter.24
  465.9 31.2 all-gather.20
  501.0 9.3 reduce-scatter.30
  591.8 63.0 reduce-scatter.38
  676.7 10.5 all-gather.22
  689.5 53.3 reduce-scatter.40
  745.0 68.5 reduce-scatter.36
  815.9 44.0 reduce-scatter.34
  862.9 44.9 reduce-scatter.32
  915.5 128.8 all-reduce.9
where the time goes:
time: 1070 us; the launch traced here: 1060 us
  waiting for transfers between devices  704 us (66%)
  matrix products  136 us (13%)
  blocking collectives  98.6 us (9%)
  other arithmetic  51.1 us (5%)
  local copies, waits for them, and re-layouts  47.7 us (4%)
  between operations  15.6 us (1%)
    reduce_scatter x4, waiting for transfers between devices, reduce_rows(): return lax.psum_scatter(partial_sum, 'row', scatter_dimension=0, tiled=True)  174 us
    psum x1, waiting for transfers between devices, shards(): lax.psum((col_place(first_gain_part), col_place(first_shift_part), query_...  129 us
    all_gather x4, waiting for transfers between devices, spread_rows(): return lax.all_gather(own_part, 'row', axis=0, tiled=True)  115 us
    unnamed x24, waiting for transfers between devices  99.6 us
    reduce_scatter x4, waiting for transfers between devices, reduce_cols(): return lax.psum_scatter(partial_sum, 'col', scatter_dimension=0, tiled=True)  47.5 us
    all_gather x1, waiting for transfers between devices, gather_keys(): return lax.all_gather(own_part, ('row', 'col'), axis=0, tiled=True)  45.9 us
    reduce_scatter x1, waiting for transfers between devices, shards(): lax.psum_scatter(triple_grad.astype(jnp.bfloat16), 'dp', scatter_dimensio...  39.6 us
    unnamed x1, blocking collectives  36.1 us
  transfers between devices with their start and end apart: 23, of which 21 were waited for; matrix products, arithmetic and copies ran while one was open for 11% of the time, Pallas kernels for 0%

commit v1 on v0

--- a/solution.py
+++ b/solution.py
@@ -11,6 +11,24 @@
 NEG = -1e30
 
 
+def collect(array, axis, dim):
+    ways, here, step = (lax.axis_size(axis), lax.axis_index(axis), array.shape[dim])
+    dims = [n * ways if d == dim else n for d, n in enumerate(array.shape)]
+    full = lax.dynamic_update_slice_in_dim(
+        jnp.zeros(dims, array.dtype), array, here * step, axis=dim
+    )
+    going_up = going_down = array
+    for far in range(1, ways // 2 + 1):
+        going_up = lax.ppermute(going_up, axis, [(d, (d + 1) % ways) for d in range(ways)])
+        full = lax.dynamic_update_slice_in_dim(full, going_up, (here - far) % ways * step, axis=dim)
+        if 2 * far < ways:
+            going_down = lax.ppermute(going_down, axis, [(d, (d - 1) % ways) for d in range(ways)])
+            full = lax.dynamic_update_slice_in_dim(
+                full, going_down, (here + far) % ways * step, axis=dim
+            )
+    return full
+
+
 def gelu_tanh(values):
     return (
         0.5
@@ -20,7 +38,7 @@
 
 
 def spread_rows(own_part):
-    return lax.all_gather(own_part, "row", axis=0, tiled=True)
+    return collect(own_part, "row", 0)
 
 
 def reduce_cols(partial_sum):

time: 1070 us -> 1050 us (0.981)
  waiting for transfers between devices: 704 us -> 658 us
  starting transfers between devices: 9.8 us -> 24.7 us
    ppermute x0 -> x12, waiting for transfers between devices: none -> 120 us  [the longest x8 80.1 us: collect(): lax.ppermute(going_up, axis, [(d, (d + 1) % ways) for d in range(ways)])]
    all_gather x4 -> x0, waiting for transfers between devices: 115 us -> none  [spread_rows(): return lax.all_gather(own_part, 'row', axis=0, tiled=True)]
    reduce_scatter x4, waiting for transfers between devices: 174 us -> 137 us  [reduce_rows(): return lax.psum_scatter(partial_sum, 'row', scatter_dimension=0, tiled=True)]
    ppermute x0 -> x12, starting transfers between devices: none -> 13.6 us  [the longest x8 6.93 us: collect(): lax.ppermute(going_up, axis, [(d, (d + 1) % ways) for d in range(ways)])]
    reduce_scatter x4, waiting for transfers between devices: 47.5 us -> 35.8 us  [reduce_cols(): return lax.psum_scatter(partial_sum, 'col', scatter_dimension=0, tiled=True)]
    unnamed x85 -> x91, local copies, waits for them, and re-layouts: 32.7 us -> 35.4 us
    unnamed x24 -> x20, waiting for transfers between devices: 99.6 us -> 98.9 us
  transfers between devices with their start and end apart: 23 -> 31, of which waited for: 21 -> 28; matrix products, arithmetic and copies ran while one was open for 11% -> 11% of each run, Pallas kernels for 0% -> 0%
where the time goes in v1:
time: 1050 us; the launch traced here: 1040 us
  waiting for transfers between devices  658 us (63%)
  matrix products  133 us (13%)
  blocking collectives  97.7 us (9%)
  local copies, waits for them, and re-layouts  57.6 us (5%)
  other arithmetic  51.5 us (5%)
  starting transfers between devices  24.7 us (2%)
  between operations  15.4 us (1%)
    reduce_scatter x4, waiting for transfers between devices, reduce_rows(): return lax.psum_scatter(partial_sum, 'row', scatter_dimension=0, tiled=True)  137 us
    psum x1, waiting for transfers between devices, shards(): lax.psum((col_place(first_gain_part), col_place(first_shift_part), query_...  128 us
    unnamed x20, waiting for transfers between devices  98.9 us
    ppermute x8, waiting for transfers between devices, collect(): lax.ppermute(going_up, axis, [(d, (d + 1) % ways) for d in range(ways)])  80.1 us
    all_gather x1, waiting for transfers between devices, gather_keys(): return lax.all_gather(own_part, ('row', 'col'), axis=0, tiled=True)  45.9 us
    ppermute x4, waiting for transfers between devices, collect(): lax.ppermute(going_down, axis, [(d, (d - 1) % ways) for d in range(ways)])  40.3 us
    reduce_scatter x1, waiting for transfers between devices, shards(): lax.psum_scatter(triple_grad.astype(jnp.bfloat16), 'dp', scatter_dimensio...  38.3 us
    reduce_scatter x4, waiting for transfers between devices, reduce_cols(): return lax.psum_scatter(partial_sum, 'col', scatter_dimension=0, tiled=True)  35.8 us
  transfers between devices with their start and end apart: 31, of which 28 were waited for; matrix products, arithmetic and copies ran while one was open for 11% of the time, Pallas kernels for 0%

profile of v1, /device:TPU:8, one launch (start us, length us, event | category | flops | bytes accessed | tf_op | source)
XLA Modules:
  0.0 1038.0 jit_solution(7015702033414544385)
XLA Ops:
  19.0 10.3 collective-permute-done
  55.9 12.5 %reduce-scatter.19.cloned.1.call-done = f32[512,1200]{0,1:T(8,128)} async-done(((f32[1024,1200]{0,1:T(8,128)}), f32[512,1200]{0,1:T(8,128)}) %reduce-scatter.19.cloned.1.call-update) | async-done | bytes 2457616 | tf_op jit(solution)/shard_map/reduce_scatter | solution.py:45
  70.3 20.1 %all_to_all.70 = bf16[4,128,1200]{1,2,0:T(8,128)(2,1)S(1)} all-to-all(bf16[4,128,1200]{1,2,0:T(8,128)(2,1)S(1)} %copy_bitcast_fusion.1), channel_id=1, replica_groups=mesh['dp'=4,'row'=4,'col'=2] {'row'}, dimensions={0} | all-to-all | bytes 2457600 | tf_op jit(solution)/shard_map/all_to_all | solution.py:57
  93.6 45.9 %all-gather.5.cloned.1.call-done = bf16[1024,3200]{0,1:T(8,128)(2,1)} async-done(((bf16[128,3200]{0,1:T(8,128)(2,1)}), bf16[1024,3200]{0,1:T(8,128)(2,1)}) %all-gather.5.cloned.1.call-update) | async-done | bytes 6553616 | tf_op jit(solution)/shard_map/all_gather | solution.py:65
  146.0 23.4 %while.28 = (s32[]{:T(128)}, bf16[5,128,5,64]{1,3,2,0:T(8,128)(2,1)S(1)}, f32[5,5,128]{2,1,0:T(8,128)S(1)}, bf16[5,1024,5,64]{1,3,2,0:T(8,128)(2,1)}, bf16[5,128...) while((s32[]{:T(128)}, ...), condition=%wide.region_8.9_spmd.clone, body=%wide.region_5.8_spmd.clone.sunk | while | flops 175414656 | bytes 9902705 | solution.py:120
  169.5 10.8 %all_to_all.71 = bf16[128,4,400]{0,2,1:T(8,128)(2,1)S(1)} all-to-all(bf16[128,4,400]{0,2,1:T(8,128)(2,1)S(1)} %bitcast.232), channel_id=1, replica_groups=mesh['dp'=4,'row'=4,'col'=2] {'row'}, dimensions={1} | all-to-all | bytes 819200 | tf_op jit(solution)/shard_map/all_to_all | solution.py:61
  190.3 15.8 %collective-permute-done.6 = bf16[256,800]{0,1:T(8,128)(2,1)S(1)} collective-permute-done((bf16[256,800]{0,1:T(8,128)(2,1)S(1)}, bf16[256,800]{0,1:T(8,128)(2,1)S(1)}, u32[]{:S(2)}, u32[]{:S(2)}) %collective-permute-start.6) | collective-permute-done | bytes 409632 | tf_op jit(solution)/shard_map/ppermute | solution.py:22
  206.3 16.4 %collective-permute-done.7 = bf16[256,800]{0,1:T(8,128)(2,1)S(1)} collective-permute-done((bf16[256,800]{0,1:T(8,128)(2,1)S(1)}, bf16[256,800]{0,1:T(8,128)(2,1)S(1)}, u32[]{:S(2)}, u32[]{:S(2)}) %collective-permute-start.7) | collective-permute-done | bytes 409632 | tf_op jit(solution)/shard_map/ppermute | solution.py:25
  222.8 12.0 %collective-permute-done.8 = bf16[256,800]{0,1:T(8,128)(2,1)S(1)} collective-permute-done((bf16[256,800]{0,1:T(8,128)(2,1)S(1)}, bf16[256,800]{0,1:T(8,128)(2,1)S(1)}, u32[]{:S(2)}, u32[]{:S(2)}) %collective-permute-start.8) | collective-permute-done | bytes 409632 | tf_op jit(solution)/shard_map/ppermute | solution.py:22
  257.4 10.3 collective-permute-done.3
  292.2 13.8 %reduce-scatter.23.cloned.1.call-done = f32[512,1600]{0,1:T(8,128)} async-done(((f32[1024,1600]{0,1:T(8,128)}), f32[512,1600]{0,1:T(8,128)}) %reduce-scatter.23.cloned.1.call-update) | async-done | bytes 3276816 | tf_op jit(solution)/shard_map/reduce_scatter | solution.py:45
  313.3 12.8 %all-gather.9.cloned.1.call-done = bf16[1024,1600]{0,1:T(8,128)(2,1)} async-done(((bf16[512,1600]{0,1:T(8,128)(2,1)}), bf16[1024,1600]{0,1:T(8,128)(2,1)}) %all-gather.9.cloned.1.call-update) | async-done | bytes 3276816 | tf_op jit(solution)/shard_map/all_gather | solution.py:49
  348.8 41.3 %reduce-scatter.29.cloned.1.call-done = f32[256,800]{0,1:T(8,128)} async-done(((f32[1024,800]{0,1:T(8,128)}), f32[256,800]{0,1:T(8,128)}) %reduce-scatter.29.cloned.1.call-update) | async-done | bytes 819216 | tf_op jit(solution)/shard_map/reduce_scatter | solution.py:53
  394.2 43.9 %reduce-scatter.25.cloned.1.call-done = f32[256,800]{0,1:T(8,128)} async-done(((f32[1024,800]{0,1:T(8,128)}), f32[256,800]{0,1:T(8,128)}) %reduce-scatter.25.cloned.1.call-update) | async-done | bytes 819216 | tf_op jit(solution)/shard_map/reduce_scatter | solution.py:53
  444.1 10.3 collective-permute-done.9
  495.3 55.7 %while.29 = (s32[]{:T(128)}, f32[5,128,5,64]{1,3,2,0:T(8,128)}, bf16[5,1024,5,64]{1,3,2,0:T(8,128)(2,1)}, bf16[5,1024,5,64]{1,3,2,0:T(8,128)(2,1)}, bf16[5,1024,...) while((s32[]{:T(128)}, f32[5,128,5,64]{1,3,2,0:T(8,128)}, ...), condition=%wide.region_25.26_spmd.clone, body=%wide.region_23.25_spmd.clone.sunk | while | flops 426909056 | bytes 17467028 | solution.py:160
  568.2 61.9 %reduce-scatter.39.cloned.1.call-done = bf16[128,3200]{1,0:T(8,128)(2,1)} async-done(((bf16[1024,3200]{1,0:T(8,128)(2,1)}), bf16[128,3200]{1,0:T(8,128)(2,1)}) %reduce-scatter.39.cloned.1.call-update) | async-done | bytes 819216
  631.9 18.8 %all_to_all.72 = bf16[128,4,1200]{0,2,1:T(8,128)(2,1)S(1)} all-to-all(bf16[128,4,1200]{0,2,1:T(8,128)(2,1)S(1)} %bitcast.226), channel_id=1, replica_groups=mesh['dp'=4,'row'=4,'col'=2] {'row'}, dimensions={1} | all-to-all | bytes 2457600 | tf_op jit(solution)/shard_map/all_to_all | solution.py:61
  682.2 36.1 %reduce-scatter.41.cloned.1.call-done = bf16[200,1600]{1,0:T(8,128)(2,1)} async-done(((bf16[800,1600]{1,0:T(8,128)(2,1)}), bf16[200,1600]{1,0:T(8,128)(2,1)}) %reduce-scatter.41.cloned.1.call-update) | async-done | bytes 640016
  722.4 34.7 %fusion.4 = bf16[112,800]{1,0:T(8,128)(2,1)S(1)} fusion(bf16[400,800]{1,0:T(8,128)(2,1)} %convolution_convert_fusion.3), kind=kCustom, calls=%all-reduce-scatter | all-reduce-scatter fusion | flops 358401 | bytes 819712
  763.6 25.3 %reduce-scatter.37.cloned.1.call-done = bf16[400,800]{1,0:T(8,128)(2,1)} async-done(((bf16[1600,800]{1,0:T(8,128)(2,1)}), bf16[400,800]{1,0:T(8,128)(2,1)}) %reduce-scatter.37.cloned.1.call-update) | async-done | bytes 640016 | tf_op jit(solution)/shard_map/reduce_scatter | solution.py:339
  797.0 38.3 %reduce-scatter.35.cloned.1.call-done = bf16[200,1200]{1,0:T(8,128)(2,1)} async-done(((bf16[800,1200]{1,0:T(8,128)(2,1)}), bf16[200,1200]{1,0:T(8,128)(2,1)}) %reduce-scatter.35.cloned.1.call-update) | async-done | bytes 480016 | tf_op jit(solution)/shard_map/reduce_scatter | solution.py:348
  837.5 45.7 %reduce-scatter.33.cloned.1.call-done = f32[256,800]{0,1:T(8,128)} async-done(((f32[1024,800]{0,1:T(8,128)}), f32[256,800]{0,1:T(8,128)}) %reduce-scatter.33.cloned.1.call-update) | async-done | bytes 819216 | tf_op jit(solution)/shard_map/reduce_scatter | solution.py:53
  891.1 128.4 %all-reduce.10.cloned.1.call-done = (f32[1600]{0:T(1024)}, f32[1600]{0:T(1024)}, f32[1600]{0:T(1024)}, f32[1600]{0:T(1024)}, f32[1600]{0:T(1024)}, /*index=5*/f3...) async-done(((f32[1600]{0:T(1024)}, f32[1600]{0:T(1024)}, f32[1600]{0:T(1024)}, f32[1600]{0:T(1024)}, f32[1600]{0:T(1024)}, /*index=5*/f32[1600]{0:T(1024)}, ...) | async-done | bytes 76816 | tf_op jit(solution)/shard_map/psum | solution.py:365
  (315 shorter events, 356.8 us)
Async XLA Ops:
  7.2 61.2 %reduce-scatter.19.cloned.1.call-start = ((), (), s32[]{:S(2)}) async-start(), calls=%async_computation.16 | async-start | bytes 7372800 | tf_op jit(solution)/shard_map/reduce_scatter | solution.py:45
  17.6 20.7 %collective-permute-start.1 = (bf16[256,800]{0,1:T(8,128)(2,1)S(1)}, bf16[256,800]{0,1:T(8,128)(2,1)}, u32[]{:S(2)}, u32[]{:S(2)}) collective-permute-start(bf16[256,800]{0,1:T(8,128)(2,1)S(1)} %get-tuple-element.326), channel_id=1, source_target_pairs={{0,6},{2,0},{4,2},{6,4},{1,7},{3,1},{5,3},{7,5},{8,14},{10,8},{12,... | collective-permute-start | bytes 1228808 | tf_op jit(solution)/shard_map/ppermute | solution.py:25
  55.1 84.4 %all-gather.5.cloned.1.call-start = ((), (), s32[]{:S(2)}) async-start(), calls=%async_computation.17 | async-start | bytes 7372800 | tf_op jit(solution)/shard_map/all_gather | solution.py:65
  92.4 155.9 %reduce-scatter.21.cloned.1.call-start = ((), (), s32[]{:S(2)}) async-start(), calls=%async_computation.18 | async-start | bytes 4096000 | tf_op jit(solution)/shard_map/reduce_scatter | solution.py:53
  186.4 105.8 %reduce-scatter.27.cloned.1.call-start = ((), (), s32[]{:S(2)}) async-start(), calls=%async_computation.22 | async-start | bytes 9830400 | tf_op jit(solution)/shard_map/reduce_scatter | solution.py:45
  187.3 18.7 %collective-permute-start.6 = (bf16[256,800]{0,1:T(8,128)(2,1)S(1)}, bf16[256,800]{0,1:T(8,128)(2,1)S(1)}, u32[]{:S(2)}, u32[]{:S(2)}) collective-permute-start(bf16[256,800]{0,1:T(8,128)(2,1)S(1)} %copy-done.6), channel_id=1, source_target_pairs={{0,2},{2,4},{4,6},{6,0},{1,3},{3,5},{5,7},{7,1},{8,10},{10,12},{12... | collective-permute-start | bytes 1228808 | tf_op jit(solution)/shard_map/ppermute | solution.py:22
  187.9 34.8 %collective-permute-start.7 = (bf16[256,800]{0,1:T(8,128)(2,1)S(1)}, bf16[256,800]{0,1:T(8,128)(2,1)S(1)}, u32[]{:S(2)}, u32[]{:S(2)}) collective-permute-start(bf16[256,800]{0,1:T(8,128)(2,1)S(1)} %copy-done.6), channel_id=1, source_target_pairs={{0,6},{2,0},{4,2},{6,4},{1,7},{3,1},{5,3},{7,5},{8,14},{10,8},{12,... | collective-permute-start | bytes 1228808 | tf_op jit(solution)/shard_map/ppermute | solution.py:25
  206.0 28.8 %collective-permute-start.8 = (bf16[256,800]{0,1:T(8,128)(2,1)S(1)}, bf16[256,800]{0,1:T(8,128)(2,1)S(1)}, u32[]{:S(2)}, u32[]{:S(2)}) collective-permute-start(bf16[256,800]{0,1:T(8,128)(2,1)S(1)} %collective-permute-done.6), channel_id=1, source_target_pairs={{0,2},{2,4},{4,6},{6,0},{1,3},{3,5},{5,7},{7,1},{8,10},{10,12},{12... | collective-permute-start | bytes 1228808 | tf_op jit(solution)/shard_map/ppermute | solution.py:22
  241.7 64.2 %reduce-scatter.23.cloned.1.call-start = ((), (), s32[]{:S(2)}) async-start(), calls=%async_computation.19 | async-start | bytes 9830400 | tf_op jit(solution)/shard_map/reduce_scatter | solution.py:45
  256.0 20.6 %collective-permute-start.4 = (bf16[256,800]{0,1:T(8,128)(2,1)S(1)}, bf16[256,800]{0,1:T(8,128)(2,1)S(1)}, u32[]{:S(2)}, u32[]{:S(2)}) collective-permute-start(bf16[256,800]{0,1:T(8,128)(2,1)S(1)} %get-tuple-element.323), channel_id=1, source_target_pairs={{0,6},{2,0},{4,2},{6,4},{1,7},{3,1},{5,3},{7,5},{8,14},{10,8},{12,... | collective-permute-start | bytes 1228808 | tf_op jit(solution)/shard_map/ppermute | solution.py:25
  291.4 34.8 %all-gather.9.cloned.1.call-start = ((), (), s32[]{:S(2)}) async-start(), calls=%async_computation.23 | async-start | bytes 4915200 | tf_op jit(solution)/shard_map/all_gather | solution.py:49
  312.5 28.7 %all-gather.7.cloned.1.call-start = ((), (), s32[]{:S(2)}) async-start(), calls=%async_computation.20 | async-start | bytes 4915200 | tf_op jit(solution)/shard_map/all_gather | solution.py:49
  313.2 76.9 %reduce-scatter.29.cloned.1.call-start = ((), (), s32[]{:S(2)}) async-start(), calls=%async_computation.24 | async-start | bytes 4096000 | tf_op jit(solution)/shard_map/reduce_scatter | solution.py:53
  332.9 105.3 %reduce-scatter.25.cloned.1.call-start = ((), (), s32[]{:S(2)}) async-start(), calls=%async_computation.21 | async-start | bytes 4096000 | tf_op jit(solution)/shard_map/reduce_scatter | solution.py:53
  348.0 134.4 %reduce-scatter.31.cloned.1.call-start = ((), (), s32[]{:S(2)}) async-start(), calls=%async_computation.25 | async-start | bytes 2457600 | tf_op jit(solution)/shard_map/reduce_scatter | solution.py:45
  442.6 20.5 %collective-permute-start.10 = (bf16[256,800]{0,1:T(8,128)(2,1)S(1)}, bf16[256,800]{0,1:T(8,128)(2,1)S(1)}, u32[]{:S(2)}, u32[]{:S(2)}) collective-permute-start(bf16[256,800]{0,1:T(8,128)(2,1)S(1)} %get-tuple-element.321), channel_id=1, source_target_pairs={{0,6},{2,0},{4,2},{6,4},{1,7},{3,1},{5,3},{7,5},{8,14},{10,8},{12,... | collective-permute-start | bytes 1228808 | tf_op jit(solution)/shard_map/ppermute | solution.py:25
  488.1 142.0 %reduce-scatter.39.cloned.1.call-start = ((), (), s32[]{:S(2)}) async-start(), calls=%async_computation.30 | async-start | bytes 7372800
  566.9 100.8 %all-gather.11.cloned.1.call-start = ((), (), s32[]{:S(2)}) async-start(), calls=%async_computation.26 | async-start | bytes 3686400 | tf_op jit(solution)/shard_map/all_gather | solution.py:49
  651.8 66.4 %reduce-scatter.41.cloned.1.call-start = ((), (), s32[]{:S(2)}) async-start(), calls=%async_computation.31 | async-start | bytes 3328000
  659.0 129.9 %reduce-scatter.37.cloned.1.call-start = ((), (), s32[]{:S(2)}) async-start(), calls=%async_computation.29 | async-start | bytes 3584000 | tf_op jit(solution)/shard_map/reduce_scatter | solution.py:339
  667.7 167.6 %reduce-scatter.35.cloned.1.call-start = ((), (), s32[]{:S(2)}) async-start(), calls=%async_computation.28 | async-start | bytes 2560000 | tf_op jit(solution)/shard_map/reduce_scatter | solution.py:348
  673.7 209.5 %reduce-scatter.33.cloned.1.call-start = ((), (), s32[]{:S(2)}) async-start(), calls=%async_computation.27 | async-start | bytes 4096000 | tf_op jit(solution)/shard_map/reduce_scatter | solution.py:53
  680.0 339.5 %all-reduce.10.cloned.1.call-start = ((), (), s32[]{:S(2)}) async-start(), calls=%async_computation.32 | async-start | bytes 188416 | tf_op jit(solution)/shard_map/psum | solution.py:365
  757.1 35.2 %collective-permute-start.12 = (bf16[36,800]{1,0:T(8,128)(2,1)S(1)}, bf16[36,800]{1,0:T(8,128)(2,1)S(1)}, u32[]{:S(2)}, u32[]{:S(2)}) collective-permute-start(bf16[36,800]{1,0:T(8,128)(2,1)S(1)} %slice.31), channel_id=1, source_target_pairs={{0,8},{8,16},{16,24},{1,9},{9,17},{17,25},{2,10},{10,18},{18,26},{... | collective-permute-start | bytes 172808
  (45 other events, 1543.2 us)
Sparse Core Ops, SparseCore 0:
  55.2 13.1 reduce-scatter.18
  92.5 46.9 all-gather.4
  186.5 61.7 reduce-scatter.20
  250.4 14.4 reduce-scatter.26
  291.5 14.4 reduce-scatter.22
  312.6 13.4 all-gather.8
  327.7 13.4 all-gather.6
  344.2 45.8 reduce-scatter.28
  393.1 44.9 reduce-scatter.24
  473.1 9.3 reduce-scatter.30
  567.1 62.9 reduce-scatter.38
  652.0 10.6 all-gather.10
  664.9 53.3 reduce-scatter.40
  720.4 68.4 reduce-scatter.36
  791.1 44.0 reduce-scatter.34
  838.1 45.0 reduce-scatter.32
  890.6 128.8 all-reduce.9
